TPU v7x, 32 devices: a whole 2x2x4 slice. The times are simulated.
32 devices in a mesh: seq: 2 (over x), tensor: 4 (over z), bucket: 4 (over y, core).
Axes of the slice: x: 2, y: 2, z: 4, core: 2. Of those that a mesh axis runs over, the one named last changes fastest.
Arguments:
- queries: bfloat16 [4, 1024, 3072], P('bucket', ('seq', 'tensor')), may hold values from -6 to 6
- keys: bfloat16 [4, 1024, 3072], P('bucket', ('seq', 'tensor')), may hold values from -6 to 6
- values: bfloat16 [4, 1024, 3072], P('bucket', ('seq', 'tensor')), may hold values from -6 to 6
- lengths: int32 [4], P('bucket'), may hold values from 256 to 1024, as said below
- out_weight: bfloat16 [3072, 3072], P(('seq', 'bucket'), 'tensor'), may hold values from -0.109375 to 0.109375
Outputs:
- projected: bfloat16 [4, 1024, 3072], P('bucket', ('seq', 'tensor'))
Inputs may be any that keep to these rules, and one draw needn't show every extreme that they name: `lengths`: each bucket has 256 to 1024 live tokens, and at least one bucket has all 1024.
All inputs are finite; a program needn't handle non-finite values.
Results may differ from a plain program's by a relative error of at most 0.018.
Values may be sent and summed in bfloat16 or wider, within the bound.
No kernel may reach another device: no remote copies, remote signals or barrier semaphores. Data moves between devices by JAX's collectives and lax.ppermute only.
A program may use at most 128 MiB of HBM per device.

v0:
```python
import jax
import jax.numpy as jnp
from jax import lax
from jax.sharding import PartitionSpec as P

HS = 128
MASKED_SCORE = -1e30


def shards(queries, keys, values, lengths, out_weight):
    tok_rows = queries.shape[1]
    n_tensor = lax.axis_size("tensor")
    tensor_index = lax.axis_index("tensor")
    live_len = lengths[0]
    local_q, local_k, local_v = (
        lax.all_to_all(queries[0], "seq", split_axis=1, concat_axis=0, tiled=True),
        lax.all_to_all(keys[0], "seq", split_axis=1, concat_axis=0, tiled=True),
        lax.all_to_all(values[0], "seq", split_axis=1, concat_axis=0, tiled=True),
    )
    row_count, col_count = local_q.shape
    head_count = col_count // HS
    query_heads = local_q.reshape(row_count, head_count, HS)

    def spots(first_row, total_rows):
        index_row = first_row + jnp.arange(total_rows, dtype=jnp.int32)
        owner = index_row // row_count
        within = index_row % row_count
        return (within // tok_rows * n_tensor + owner) * tok_rows + within % tok_rows

    query_usable = spots(tensor_index * row_count, row_count) < live_len
    initial = (
        jnp.full((row_count, head_count), MASKED_SCORE, jnp.float32),
        jnp.zeros((row_count, head_count), jnp.float32),
        jnp.zeros((row_count, head_count, HS), jnp.float32),
    )
    carried = initial
    first_row = jnp.int32(0)
    key_rows = lax.all_gather(local_k, "tensor", axis=0, tiled=True)
    value_rows = lax.all_gather(local_v, "tensor", axis=0, tiled=True)
    for offset in range(key_rows.shape[0] // row_count):
        row_peak, row_sum, accumulated = carried
        key_tile = key_rows[offset * row_count : (offset + 1) * row_count].reshape(
            row_count, head_count, HS
        )
        value_tile = value_rows[offset * row_count : (offset + 1) * row_count].reshape(
            row_count, head_count, HS
        )
        key_usable = spots(first_row + offset * row_count, row_count) < live_len
        scores = jnp.einsum(
            "qhd,khd->qhk", query_heads, key_tile, preferred_element_type=jnp.float32
        ) * HS ** (-0.5)
        scores = jnp.where(key_usable[None, None, :], scores, MASKED_SCORE)
        peak_new = jnp.maximum(row_peak, jnp.max(scores, axis=-1))
        exponent = jnp.where(key_usable[None, None, :], jnp.exp(scores - peak_new[..., None]), 0.0)
        rescale = jnp.exp(row_peak - peak_new)
        accumulated = accumulated * rescale[..., None] + jnp.einsum(
            "qhk,khd->qhd",
            exponent.astype(jnp.bfloat16),
            value_tile,
            preferred_element_type=jnp.float32,
        )
        carried = (peak_new, row_sum * rescale + jnp.sum(exponent, axis=-1), accumulated)
    row_peak, row_sum, accumulated = carried
    attended = accumulated / row_sum[..., None]
    mixed = jnp.where(query_usable[:, None], attended.reshape(row_count, col_count), 0.0).astype(
        jnp.bfloat16
    )
    restored = lax.all_to_all(mixed, "seq", split_axis=0, concat_axis=1, tiled=True)
    wide_weight = lax.all_gather(out_weight, "tensor", axis=1, tiled=True)
    summed = jnp.dot(
        restored,
        lax.all_gather(wide_weight, ("seq", "bucket"), axis=0, tiled=True),
        preferred_element_type=jnp.float32,
    )
    return summed.astype(jnp.bfloat16)[None]


def solution(mesh):
    in_specs = (
        P("bucket", ("seq", "tensor"), None),
        P("bucket", ("seq", "tensor"), None),
        P("bucket", ("seq", "tensor"), None),
        P("bucket"),
        P(("seq", "bucket"), "tensor"),
    )
    out_specs = P("bucket", ("seq", "tensor"), None)
    return jax.shard_map(shards, mesh=mesh, in_specs=in_specs, out_specs=out_specs, check_vma=False)
```

profile of v0, /device:TPU:0, one launch (start us, length us, event | category | flops | bytes accessed | tf_op | source)
XLA Modules:
  0.0 309.9 jit_solution(5005568359367810147)
XLA Ops:
  7.3 1.5 copy.68
  8.8 14.8 %all_to_all.70 = bf16[128,2,1536]{0,2,1:T(8,128)(2,1)S(1)} all-to-all(bf16[128,2,1536]{0,2,1:T(8,128)(2,1)S(1)} %bitcast.125), channel_id=1, replica_groups=mesh['seq'=2,'tensor'=4,'bucket'=4] {'seq'}, dimensions={1} | all-to-all | bytes 1572864 | tf_op jit(solution)/shard_map/all_to_all | solution.py:17
  25.3 12.5 %all_to_all.71 = bf16[128,2,1536]{0,2,1:T(8,128)(2,1)S(1)} all-to-all(bf16[128,2,1536]{0,2,1:T(8,128)(2,1)S(1)} %bitcast.126), channel_id=1, replica_groups=mesh['seq'=2,'tensor'=4,'bucket'=4] {'seq'}, dimensions={1} | all-to-all | bytes 1572864 | tf_op jit(solution)/shard_map/all_to_all | solution.py:18
  39.0 22.6 %all-gather.9.cloned.1.call-done = bf16[384,3072]{1,0:T(8,128)(2,1)} async-done(((bf16[384,768]{1,0:T(8,128)(2,1)}), bf16[384,3072]{1,0:T(8,128)(2,1)}) %all-gather.9.cloned.1.call-update) | async-done | bytes 2359312 | tf_op jit(solution)/shard_map/all_gather | solution.py:69
  62.8 3.5 %all-to-all-start.1 = ((bf16[128,2,1536]{0,2,1:T(8,128)(2,1)}), bf16[128,2,1536]{0,2,1:T(8,128)(2,1)S(1)}, u32[]{:S(2)}, u32[]{:S(2)}) async-start(bf16[128,2,1536]{0,2,1:T(8,128)(2,1)} %bitcast.5), calls=%async_computation.1 | async-start | bytes 1572864 | tf_op jit(solution)/shard_map/all_to_all | solution.py:16
  67.1 10.2 %all-to-all-done.1 = bf16[128,2,1536]{0,2,1:T(8,128)(2,1)S(1)} async-done(((bf16[128,2,1536]{0,2,1:T(8,128)(2,1)}), bf16[128,2,1536]{0,2,1:T(8,128)(2,1)S(1)}, u32[]{:S(2)}, u32[]{:S(2)}) %all-to-all-start.1) | async-done | bytes 786464 | tf_op jit(solution)/shard_map/all_to_all | solution.py:16
  77.3 6.7 %copy.72 = bf16[2,128,1536]{1,0,2:T(2,128)(2,1)S(1)} copy(bf16[2,128,1536]{1,2,0:T(8,128)(2,1)S(1)} %bitcast.122) | data formatting | bytes 1572864 | tf_op jit(solution)/shard_map/all_to_all | solution.py:16
  84.4 41.0 %all-gather.5.cloned.1.call-done = bf16[1024,1536]{1,0:T(8,128)(2,1)} async-done(((bf16[256,1536]{1,0:T(8,128)(2,1)}), bf16[1024,1536]{1,0:T(8,128)(2,1)}) %all-gather.5.cloned.1.call-update) | async-done | bytes 3145744 | tf_op jit(solution)/shard_map/all_gather | solution.py:38
  125.4 2.9 fusion.89
  128.4 1.2 copy.70
  130.1 1.4 copy.80
  131.5 57.6 %all-gather.7.cloned.1.call-done = bf16[1024,1536]{1,0:T(8,128)(2,1)} async-done(((bf16[256,1536]{1,0:T(8,128)(2,1)}), bf16[1024,1536]{1,0:T(8,128)(2,1)}) %all-gather.7.cloned.1.call-update) | async-done | bytes 3145744 | tf_op jit(solution)/shard_map/all_gather | solution.py:39
  189.1 3.6 %fusion.88 = (bf16[256,1536]{1,0:T(8,128)(2,1)}, bf16[256,1536]{1,0:T(8,128)(2,1)}, bf16[256,1536]{1,0:T(8,128)(2,1)}, bf16[256,1536]{1,0:T(8,128)(2,1)}) fusion(bf16[1024,1536]{1,0:T(8,128)(2,1)} %all-gather.7.cloned.1.call-done), kind=kLoop, calls=%fused_computation.155 | loop fusion | bytes 6291456 | tf_op jit(solution)/shard_map/slice | solution.py:45
  192.7 2.3 copy.83
  195.0 2.5 copy.89
  197.5 2.4 copy.95
  199.9 2.5 copy.77
  202.4 1.9 bitcast_reduce_fusion.3
  211.6 1.4 fusion.19
  212.9 1.2 fusion.17
  214.2 3.0 fusion.25
  218.6 16.7 %all_to_all.72 = bf16[2,128,1536]{1,2,0:T(8,128)(2,1)S(1)} all-to-all(bf16[2,128,1536]{1,2,0:T(8,128)(2,1)S(1)} %copy.99), channel_id=1, replica_groups=mesh['seq'=2,'tensor'=4,'bucket'=4] {'seq'}, dimensions={0} | all-to-all | bytes 1572864 | tf_op jit(solution)/shard_map/all_to_all | solution.py:68
  235.3 58.3 %all-gather.11.cloned.1.call-done = bf16[3072,3072]{1,0:T(8,128)(2,1)} async-done(((bf16[384,3072]{1,0:T(8,128)(2,1)}), bf16[3072,3072]{1,0:T(8,128)(2,1)}) %all-gather.11.cloned.1.call-update) | async-done | bytes 18874384 | tf_op jit(solution)/shard_map/all_gather | solution.py:72
  293.5 9.9 %fusion = bf16[1,128,3072]{2,1,0:T(8,128)(2,1)} fusion(bf16[128,3072]{0,1:T(8,128)(2,1)S(1)} %bitcast.115, bf16[3072,3072]{1,0:T(8,128)(2,1)} %all-gather.11.cloned.1.call-done), kind=kOutput, calls=%fused_computation.1 | convolution fusion | flops 2416312320 | bytes 20447232 | tf_op jit(solution)/shard_map/dot_general | solution.py:70
  (44 shorter events, 14.3 us)
Async XLA Ops:
  6.5 18.3 %copy-start = (bf16[1,128,3072]{2,1,0:T(8,128)(2,1)S(1)}, bf16[1,128,3072]{2,1,0:T(8,128)(2,1)}, u32[]{:S(2)}) copy-start(bf16[1,128,3072]{2,1,0:T(8,128)(2,1)} %param.7) | copy-start | bytes 2359300
  6.5 55.1 %all-gather.9.cloned.1.call-start = ((), (), s32[]{:S(2)}) async-start(), calls=%async_computation.6 | async-start | bytes 2949120 | tf_op jit(solution)/shard_map/all_gather | solution.py:69
  7.3 118.2 %all-gather.5.cloned.1.call-start = ((), (), s32[]{:S(2)}) async-start(), calls=%async_computation.4 | async-start | bytes 3932160 | tf_op jit(solution)/shard_map/all_gather | solution.py:38
  24.8 164.3 %all-gather.7.cloned.1.call-start = ((), (), s32[]{:S(2)}) async-start(), calls=%async_computation.5 | async-start | bytes 3932160 | tf_op jit(solution)/shard_map/all_gather | solution.py:39
  25.3 36.4 %copy-start.1 = (bf16[1,128,3072]{2,1,0:T(8,128)(2,1)S(1)}, bf16[1,128,3072]{2,1,0:T(8,128)(2,1)}, u32[]{:S(2)}) copy-start(bf16[1,128,3072]{2,1,0:T(8,128)(2,1)} %param.5) | copy-start | bytes 2359300
  39.0 254.6 %all-gather.11.cloned.1.call-start = ((), (), s32[]{:S(2)}) async-start(), calls=%async_computation.7 | async-start | bytes 21233664 | tf_op jit(solution)/shard_map/all_gather | solution.py:72
  62.8 14.4 %all-to-all-start.1 = ((bf16[128,2,1536]{0,2,1:T(8,128)(2,1)}), bf16[128,2,1536]{0,2,1:T(8,128)(2,1)S(1)}, u32[]{:S(2)}, u32[]{:S(2)}) async-start(bf16[128,2,1536]{0,2,1:T(8,128)(2,1)} %bitcast.5), calls=%async_computation.1 | async-start | bytes 1572864 | tf_op jit(solution)/shard_map/all_to_all | solution.py:16
  208.6 1.7 copy-start.5
  210.4 1.2 copy-start.4
  211.6 1.4 copy-start.3
  212.9 1.2 copy-start.2
Sparse Core Ops, SparseCore 0:
  8.9 52.6 all-gather.8
  63.2 62.1 all-gather.4
  127.0 62.0 all-gather.6
  190.9 102.6 all-gather.10
where the time goes:
time: 311 us; the launch traced here: 310 us
  waiting for transfers between devices  190 us (61%)
  blocking collectives  44 us (14%)
  local copies, waits for them, and re-layouts  32.5 us (10%)
  matrix products  21.1 us (7%)
  between operations  14.1 us (5%)
  other arithmetic  4.22 us (1%)
  starting transfers between devices  3.66 us (1%)
    all_gather x1, waiting for transfers between devices, shards(): lax.all_gather(wide_weight, ('seq', 'bucket'), axis=0, tiled=True)  58.3 us
    all_gather x1, waiting for transfers between devices, shards(): value_rows = lax.all_gather(local_v, 'tensor', axis=0, tiled=True)  57.6 us
    all_gather x1, waiting for transfers between devices, shards(): key_rows = lax.all_gather(local_k, 'tensor', axis=0, tiled=True)  41 us
    all_gather x1, waiting for transfers between devices, shards(): wide_weight = lax.all_gather(out_weight, 'tensor', axis=1, tiled=True)  22.6 us
    all_to_all x1, blocking collectives, shards(): lax.all_to_all(mixed, 'seq', split_axis=0, concat_axis=1, tiled=True)  16.7 us
    all_to_all x1, blocking collectives, shards(): lax.all_to_all(keys[0], 'seq', split_axis=1, concat_axis=0, tiled=True)  14.8 us
    slice x5, local copies, waits for them, and re-layouts, shards(): value_rows[offset * row_count:(offset + 1) * row_count]  13.3 us
    all_to_all x1, blocking collectives, shards(): lax.all_to_all(values[0], 'seq', split_axis=1, concat_axis=0, tiled=True)  12.5 us
  transfers between devices with their start and end apart: 5, of which 5 were waited for; matrix products, arithmetic and copies ran while one was open for 15% of the time, Pallas kernels for 0%

commit v1 on v0

--- a/solution.py
+++ b/solution.py
@@ -35,7 +35,13 @@
     )
     carried = initial
     first_row = jnp.int32(0)
-    key_rows = lax.all_gather(local_k, "tensor", axis=0, tiled=True)
+    size = lax.axis_size("tensor")
+    held, tiles = (local_k, [local_k])
+    for _ in range(size - 1):
+        held = lax.ppermute(held, "tensor", [(i, (i + 1) % size) for i in range(size)])
+        tiles.insert(0, held)
+    row_of_blocks = jnp.concatenate(tiles, axis=0)
+    key_rows = jnp.roll(row_of_blocks, (lax.axis_index("tensor") + 1) * local_k.shape[0], axis=0)
     value_rows = lax.all_gather(local_v, "tensor", axis=0, tiled=True)
     for offset in range(key_rows.shape[0] // row_count):
         row_peak, row_sum, accumulated = carried

time: 311 us -> 285 us (0.916)
  waiting for transfers between devices: 190 us -> 138 us
  starting transfers between devices: 3.66 us -> 16.6 us
  local copies, waits for them, and re-layouts: 32.5 us -> 39.4 us
  blocking collectives: 44 us -> 50.4 us
    ppermute x0 -> x3, waiting for transfers between devices: none -> 70.4 us  [shards(): lax.ppermute(held, 'tensor', [(i, (i + 1) % size) for i in range(size)])]
    all_gather x1, waiting for transfers between devices: 57.6 us -> 0.02 us  [shards(): value_rows = lax.all_gather(local_v, 'tensor', axis=0, tiled=True)]
    all_gather x1, waiting for transfers between devices: 58.3 us -> 10.4 us  [shards(): lax.all_gather(wide_weight, ('seq', 'bucket'), axis=0, tiled=True)]
    all_gather x1 -> x0, waiting for transfers between devices: 41 us -> none  [shards(): key_rows = lax.all_gather(local_k, 'tensor', axis=0, tiled=True)]
    all_gather x1, waiting for transfers between devices: 22.6 us -> 36.6 us  [shards(): wide_weight = lax.all_gather(out_weight, 'tensor', axis=1, tiled=True)]
    ppermute x0 -> x3, starting transfers between devices: none -> 12.9 us  [shards(): lax.ppermute(held, 'tensor', [(i, (i + 1) % size) for i in range(size)])]
    all_to_all x1, waiting for transfers between devices: 10.2 us -> 19.3 us  [shards(): lax.all_to_all(queries[0], 'seq', split_axis=1, concat_axis=0, tiled=True)]
    unnamed x15 -> x34, local copies, waits for them, and re-layouts: 3.05 us -> 10.3 us
  transfers between devices with their start and end apart: 5 -> 7, of which waited for: 5 -> 5; matrix products, arithmetic and copies ran while one was open for 15% -> 18% of each run, Pallas kernels for 0% -> 0%
where the time goes in v1:
time: 285 us
  waiting for transfers between devices  138 us (48%)
  blocking collectives  50.4 us (18%)
  local copies, waits for them, and re-layouts  39.4 us (14%)
  matrix products  22.4 us (8%)
  starting transfers between devices  16.6 us (6%)
  between operations  14.1 us (5%)
  other arithmetic  4.3 us (2%)
    ppermute x3, waiting for transfers between devices, shards(): lax.ppermute(held, 'tensor', [(i, (i + 1) % size) for i in range(size)])  70.4 us
    all_gather x1, waiting for transfers between devices, shards(): wide_weight = lax.all_gather(out_weight, 'tensor', axis=1, tiled=True)  36.6 us
    all_to_all x1, blocking collectives, shards(): lax.all_to_all(mixed, 'seq', split_axis=0, concat_axis=1, tiled=True)  22.1 us
    all_to_all x1, waiting for transfers between devices, shards(): lax.all_to_all(queries[0], 'seq', split_axis=1, concat_axis=0, tiled=True)  19.3 us
    all_to_all x1, blocking collectives, shards(): lax.all_to_all(values[0], 'seq', split_axis=1, concat_axis=0, tiled=True)  14.9 us
    all_to_all x1, blocking collectives, shards(): lax.all_to_all(keys[0], 'seq', split_axis=1, concat_axis=0, tiled=True)  13.3 us
    ppermute x3, starting transfers between devices, shards(): lax.ppermute(held, 'tensor', [(i, (i + 1) % size) for i in range(size)])  12.9 us
    slice x5, local copies, waits for them, and re-layouts, shards(): value_rows[offset * row_count:(offset + 1) * row_count]  12.9 us
  transfers between devices with their start and end apart: 7, of which 5 were waited for; matrix products, arithmetic and copies ran while one was open for 18% of the time, Pallas kernels for 0%

profile of v1, /device:TPU:0, one launch (start us, length us, event | category | flops | bytes accessed | tf_op | source)
XLA Modules:
  0.0 284.7 jit_solution(3637348218246623056)
XLA Ops:
  7.3 1.5 copy.75
  8.8 14.9 %all_to_all.70 = bf16[128,2,1536]{0,2,1:T(8,128)(2,1)S(1)} all-to-all(bf16[128,2,1536]{0,2,1:T(8,128)(2,1)S(1)} %bitcast.128), channel_id=1, replica_groups=mesh['seq'=2,'tensor'=4,'bucket'=4] {'seq'}, dimensions={1} | all-to-all | bytes 1572864 | tf_op jit(solution)/shard_map/all_to_all | solution.py:18
  25.0 36.6 %all-gather.6.cloned.1.call-done = bf16[384,3072]{1,0:T(8,128)(2,1)} async-done(((bf16[384,768]{1,0:T(8,128)(2,1)}), bf16[384,3072]{1,0:T(8,128)(2,1)}) %all-gather.6.cloned.1.call-update) | async-done | bytes 2359312 | tf_op jit(solution)/shard_map/all_gather | solution.py:75
  62.1 13.3 %all_to_all.71 = bf16[128,2,1536]{0,2,1:T(8,128)(2,1)S(1)} all-to-all(bf16[128,2,1536]{0,2,1:T(8,128)(2,1)S(1)} %bitcast.129), channel_id=1, replica_groups=mesh['seq'=2,'tensor'=4,'bucket'=4] {'seq'}, dimensions={1} | all-to-all | bytes 1572864 | tf_op jit(solution)/shard_map/all_to_all | solution.py:17
  75.7 38.4 %collective-permute-done = bf16[256,1536]{1,0:T(8,128)(2,1)S(1)} collective-permute-done((bf16[256,1536]{1,0:T(8,128)(2,1)S(1)}, bf16[256,1536]{1,0:T(8,128)(2,1)S(1)}, u32[]{:S(2)}, u32[]{:S(2)}) %collective-permute-start) | collective-permute-done | bytes 786464 | tf_op jit(solution)/shard_map/ppermute | solution.py:41
  114.1 12.9 %collective-permute-start.1 = (bf16[256,1536]{1,0:T(8,128)(2,1)S(1)}, bf16[256,1536]{1,0:T(8,128)(2,1)S(1)}, u32[]{:S(2)}, u32[]{:S(2)}) collective-permute-start(bf16[256,1536]{1,0:T(8,128)(2,1)S(1)} %collective-permute-done), channel_id=1, source_target_pairs={{0,4},{4,8},{8,12},{12,0},{1,5},{5,9},{9,13},{13,1},{2,6},{6,10},{... | collective-permute-start | bytes 2359304 | tf_op jit(solution)/shard_map/ppermute | solution.py:41
  127.0 32.0 %collective-permute-done.1 = bf16[256,1536]{1,0:T(8,128)(2,1)S(1)} collective-permute-done((bf16[256,1536]{1,0:T(8,128)(2,1)S(1)}, bf16[256,1536]{1,0:T(8,128)(2,1)S(1)}, u32[]{:S(2)}, u32[]{:S(2)}) %collective-permute-start.1) | collective-permute-done | bytes 786464 | tf_op jit(solution)/shard_map/ppermute | solution.py:41
  159.0 2.3 copy.71
  161.3 3.6 %all-to-all-start.1 = ((bf16[128,2,1536]{0,2,1:T(8,128)(2,1)}), bf16[128,2,1536]{0,2,1:T(8,128)(2,1)S(1)}, u32[]{:S(2)}, u32[]{:S(2)}) async-start(bf16[128,2,1536]{0,2,1:T(8,128)(2,1)} %bitcast.125), calls=%async_computation.1 | async-start | bytes 1572864 | tf_op jit(solution)/shard_map/all_to_all | solution.py:16
  165.7 19.3 %all-to-all-done.1 = bf16[128,2,1536]{0,2,1:T(8,128)(2,1)S(1)} async-done(((bf16[128,2,1536]{0,2,1:T(8,128)(2,1)}), bf16[128,2,1536]{0,2,1:T(8,128)(2,1)S(1)}, u32[]{:S(2)}, u32[]{:S(2)}) %all-to-all-start.1) | async-done | bytes 786464 | tf_op jit(solution)/shard_map/all_to_all | solution.py:16
  185.0 7.2 %copy.72 = bf16[2,128,1536]{1,0,2:T(2,128)(2,1)} copy(bf16[2,128,1536]{1,2,0:T(8,128)(2,1)S(1)} %bitcast.124) | data formatting | bytes 1572864 | tf_op jit(solution)/shard_map/all_to_all | solution.py:16
  192.3 2.6 reshape.424
  200.5 1.4 copy.92
  201.9 1.9 bitcast_reduce_fusion.1
  211.9 3.6 %fusion.88 = (bf16[256,1536]{1,0:T(8,128)(2,1)}, bf16[256,1536]{1,0:T(8,128)(2,1)}, bf16[256,1536]{1,0:T(8,128)(2,1)}, bf16[256,1536]{1,0:T(8,128)(2,1)}) fusion(bf16[1024,1536]{1,0:T(8,128)(2,1)} %all-gather.4.cloned.1.call-done), kind=kLoop, calls=%fused_computation.167 | loop fusion | bytes 6291456 | tf_op jit(solution)/shard_map/slice | solution.py:51
  215.4 2.4 copy.83
  217.9 2.3 copy.89
  220.2 2.3 copy.95
  222.5 2.3 copy.77
  224.8 2.4 fusion.21
  231.5 3.0 %fusion.25 = bf16[256,12,128]{2,0,1:T(8,128)(2,1)S(1)} fusion(f32[12,256,128]{2,1,0:T(8,128)S(1)} %fusion.17, f32[12,256,128]{2,1,0:T(8,128)S(1)} %fusion.19, f32[12,256,128]{2,1,0:T(8,128)S(1)} %fusion.21, f32[256,12]{0,1:T(8,128)S(1)} %get-tuple-element.5, f32[256,12]{0,1:T(8,128)S(1)} %get-tuple-element.8, f32[256,12]{0,1:T(8,128)S(1)} %get-tuple-element.7, ...), kind=kOutput, calls=%fused_computation.35 | convolution fusion | flops 208797696 | bytes 9511168 | tf_op jit(solution)/shard_map/qhk,khd->qhd/dot_general | solution.py:62
  235.9 22.1 %all_to_all.72 = bf16[2,128,1536]{1,2,0:T(8,128)(2,1)S(1)} all-to-all(bf16[2,128,1536]{1,2,0:T(8,128)(2,1)S(1)} %copy.99), channel_id=1, replica_groups=mesh['seq'=2,'tensor'=4,'bucket'=4] {'seq'}, dimensions={0} | all-to-all | bytes 1572864 | tf_op jit(solution)/shard_map/all_to_all | solution.py:74
  257.9 10.4 %all-gather.8.cloned.1.call-done = bf16[3072,3072]{1,0:T(8,128)(2,1)} async-done(((bf16[384,3072]{1,0:T(8,128)(2,1)}), bf16[3072,3072]{1,0:T(8,128)(2,1)}) %all-gather.8.cloned.1.call-update) | async-done | bytes 18874384 | tf_op jit(solution)/shard_map/all_gather | solution.py:78
  268.3 9.9 %fusion = bf16[1,128,3072]{2,1,0:T(8,128)(2,1)} fusion(bf16[128,3072]{0,1:T(8,128)(2,1)S(1)} %bitcast.118, bf16[3072,3072]{1,0:T(8,128)(2,1)} %all-gather.8.cloned.1.call-done), kind=kOutput, calls=%fused_computation.1 | convolution fusion | flops 2416312320 | bytes 20447232 | tf_op jit(solution)/shard_map/dot_general | solution.py:76
  (67 shorter events, 21.8 us)
Async XLA Ops:
  6.5 55.1 %all-gather.6.cloned.1.call-start = ((), (), s32[]{:S(2)}) async-start(), calls=%async_computation.5 | async-start | bytes 2949120 | tf_op jit(solution)/shard_map/all_gather | solution.py:75
  7.3 204.6 %all-gather.4.cloned.1.call-start = ((), (), s32[]{:S(2)}) async-start(), calls=%async_computation.4 | async-start | bytes 3932160 | tf_op jit(solution)/shard_map/all_gather | solution.py:45
  8.8 52.9 %copy-start.8 = (bf16[1,128,3072]{2,1,0:T(8,128)(2,1)S(1)}, bf16[1,128,3072]{2,1,0:T(8,128)(2,1)}, u32[]{:S(2)}) copy-start(bf16[1,128,3072]{2,1,0:T(8,128)(2,1)} %param.6) | copy-start | bytes 2359300
  25.0 243.3 %all-gather.8.cloned.1.call-start = ((), (), s32[]{:S(2)}) async-start(), calls=%async_computation.6 | async-start | bytes 21233664 | tf_op jit(solution)/shard_map/all_gather | solution.py:78
  75.7 38.5 %collective-permute-start = (bf16[256,1536]{1,0:T(8,128)(2,1)S(1)}, bf16[256,1536]{1,0:T(8,128)(2,1)S(1)}, u32[]{:S(2)}, u32[]{:S(2)}) collective-permute-start(bf16[256,1536]{1,0:T(8,128)(2,1)S(1)} %bitcast.115), channel_id=1, source_target_pairs={{0,4},{4,8},{8,12},{12,0},{1,5},{5,9},{9,13},{13,1},{2,6},{6,10},{... | collective-permute-start | bytes 2359304 | tf_op jit(solution)/shard_map/ppermute | solution.py:41
  114.1 44.9 %collective-permute-start.1 = (bf16[256,1536]{1,0:T(8,128)(2,1)S(1)}, bf16[256,1536]{1,0:T(8,128)(2,1)S(1)}, u32[]{:S(2)}, u32[]{:S(2)}) collective-permute-start(bf16[256,1536]{1,0:T(8,128)(2,1)S(1)} %collective-permute-done), channel_id=1, source_target_pairs={{0,4},{4,8},{8,12},{12,0},{1,5},{5,9},{9,13},{13,1},{2,6},{6,10},{... | collective-permute-start | bytes 2359304 | tf_op jit(solution)/shard_map/ppermute | solution.py:41
  159.0 35.9 %collective-permute-start.2 = (bf16[256,1536]{1,0:T(8,128)(2,1)S(1)}, bf16[256,1536]{1,0:T(8,128)(2,1)}, u32[]{:S(2)}, u32[]{:S(2)}) collective-permute-start(bf16[256,1536]{1,0:T(8,128)(2,1)S(1)} %collective-permute-done.1), channel_id=1, source_target_pairs={{0,4},{4,8},{8,12},{12,0},{1,5},{5,9},{9,13},{13,1},{2,6},{6,10},{... | collective-permute-start | bytes 2359304 | tf_op jit(solution)/shard_map/ppermute | solution.py:41
  161.3 23.7 %all-to-all-start.1 = ((bf16[128,2,1536]{0,2,1:T(8,128)(2,1)}), bf16[128,2,1536]{0,2,1:T(8,128)(2,1)S(1)}, u32[]{:S(2)}, u32[]{:S(2)}) async-start(bf16[128,2,1536]{0,2,1:T(8,128)(2,1)} %bitcast.125), calls=%async_computation.1 | async-start | bytes 1572864 | tf_op jit(solution)/shard_map/all_to_all | solution.py:16
  203.9 5.9 %copy-start.2 = (f32[12,256,256]{2,1,0:T(8,128)}, f32[12,256,256]{2,1,0:T(8,128)S(1)}, u32[]{:S(2)}) copy-start(f32[12,256,256]{2,1,0:T(8,128)S(1)} %get-tuple-element.25) | copy-start | bytes 9437188
  204.7 4.1 %copy-start.4 = (f32[12,256,256]{2,1,0:T(8,128)}, f32[12,256,256]{2,1,0:T(8,128)S(1)}, u32[]{:S(2)}) copy-start(f32[12,256,256]{2,1,0:T(8,128)S(1)} %get-tuple-element.27) | copy-start | bytes 9437188
  205.6 2.2 copy-start
  206.5 4.5 %copy-start.6 = (f32[12,256,256]{2,1,0:T(8,128)}, f32[12,256,256]{2,1,0:T(8,128)S(1)}, u32[]{:S(2)}) copy-start(f32[12,256,256]{2,1,0:T(8,128)S(1)} %get-tuple-element.23) | copy-start | bytes 9437188
  215.4 9.3 %copy-start.5 = (f32[12,256,256]{2,1,0:T(8,128)S(1)}, f32[12,256,256]{2,1,0:T(8,128)}, u32[]{:S(2)}) copy-start(f32[12,256,256]{2,1,0:T(8,128)} %copy-done.4) | copy-start | bytes 9437188
  224.8 2.5 copy-start.3
  224.8 2.5 copy-start.11
  227.2 2.0 copy-start.7
  227.2 2.1 copy-start.10
  229.4 1.9 copy-start.1
  229.4 2.1 copy-start.9
Sparse Core Ops, SparseCore 0:
  8.9 52.6 all-gather.5
  63.2 88.9 all-gather.3
  154.1 114.1 all-gather.7
